TPU v7x, 256 devices: a whole 4x4x8 slice. The times are simulated.
256 devices in a mesh: section: 8 (over z), col: 32 (over y, x, core).
Axes of the slice: x: 4, y: 4, z: 8, core: 2. Of those that a mesh axis runs over, the one named last changes fastest.
Arguments:
- tiles: bfloat16 [1024, 12, 128, 128], P('col', None, 'section'), may hold values from 0.0099487305 to 1
- offsets: int32 [1024, 12], replicated, may hold values from -6 to 6, as said below
- counts: int32 [1024], replicated, may hold values from 1 to 12
- ranks: int32 [1024, 25, 128, 128], P('col', None, 'section'), may hold values from 0 to 3199, as said below
Outputs:
- pruned: bfloat16 [1024, 25, 128, 128], P('col', None, 'section')
Inputs may be any that keep to these rules, and one draw needn't show every extreme that they name: Within each panel the 12 offsets are distinct, each from -6 to 6. For every panel j and column c, ranks[j, :, c, :] holds each of 0 .. 3199 once.
All inputs are finite; a program needn't handle non-finite values.
Results may differ from a plain program's by a relative error of at most 0.001.
Values may be sent and summed in bfloat16 or wider, within the bound.
A program may use at most 128 MiB of HBM per device.

v0:
```python
import jax
import jax.numpy as jnp
from jax import lax
from jax.sharding import PartitionSpec as P

W = 6
TOPK = 256


def extended(shard, sides, width):
    for axis, dim in sides:
        count, length = (lax.axis_size(axis), shard.shape[dim])
        up = [(i, (i + 1) % count) for i in range(count - 1)]
        down = [(j, i) for i, j in up]
        last = lax.slice_in_dim(shard, length - width, length, axis=dim)
        initial = lax.slice_in_dim(shard, 0, width, axis=dim)
        before = lax.ppermute(last, axis, up)
        after = lax.ppermute(initial, axis, down)
        shard = jnp.concatenate([before, shard, after], axis=dim)
    return shard


def cut_along(shard, dim, count):
    before, after = (shard.shape[:dim], shard.shape[dim + 1 :])
    return jnp.moveaxis(shard.reshape(*before, count, -1, *after), dim, 0)


def piece_ends(length, count):
    unit = 8 if length >= 8 * count else 1
    return [length // unit * k // count * unit for k in range(1, count)]


def joined_along(tiles, dim):
    tiles = jnp.moveaxis(tiles, 0, dim)
    dims = tiles.shape
    return tiles.reshape(*dims[:dim], dims[dim] * dims[dim + 1], *dims[dim + 2 :])


def exchange_in_pieces(shard, axis, pieces, split_dim, concat_dim):
    tiles = cut_along(shard, split_dim, lax.axis_size(axis))
    split_at = max(range(1, max(2, tiles.ndim - 1)), key=lambda d: tiles.shape[d])
    outs = []
    for share in jnp.split(tiles, piece_ends(tiles.shape[split_at], pieces), axis=split_at):
        if share.size:
            outs.append(lax.all_to_all(share, axis, split_axis=0, concat_axis=0, tiled=True))
    return joined_along(jnp.concatenate(outs, axis=split_at), concat_dim)


def expand(own, own_off, own_cnt, center, global_panel, banded, band_off, band_cnt, total, bands):
    slots = own.shape[0]
    slot_ids = jnp.arange(slots, dtype=jnp.int32)
    where_at = center + W + own_off
    firsts = banded[where_at]
    first_off = band_off[where_at]
    first_cnt = band_cnt[where_at]
    row_own = global_panel + own_off
    ok_own = (slot_ids < own_cnt) & (row_own >= 0) & (row_own < total)
    row_first = row_own[:, None] + first_off
    ok_first = (slot_ids[None, :] < first_cnt[:, None]) & (row_first >= 0) & (row_first < total)
    weight = (ok_own[:, None] & ok_first).astype(jnp.float32)
    target = own_off[:, None] + first_off + 2 * W
    products = jnp.einsum("kcx,klxr->klcr", own, firsts, preferred_element_type=jnp.float32)
    weighted = products * weight[:, :, None, None]
    columns = own.shape[1]
    rows = own.shape[2]
    empty = jnp.zeros((bands, columns, rows), jnp.float32)
    return empty.at[target.reshape(-1)].add(weighted.reshape((slots * slots, columns, rows)))


def finish(expanded, rank_block):
    keep = rank_block < TOPK
    squared = jnp.where(keep, expanded * expanded, jnp.float32(0.0))
    totals = jnp.sum(squared, axis=(0, 2), keepdims=True)
    return (TOPK * squared / (totals + 1e-06)).astype(jnp.bfloat16)


def shards(tiles, offsets, counts, ranks):
    panels = tiles.shape[0]
    slots = tiles.shape[1]
    bands = ranks.shape[1]
    total = offsets.shape[0]
    first_panel = lax.axis_index("col") * panels
    pad_off = jnp.concatenate(
        [jnp.zeros((W, slots), jnp.int32), offsets, jnp.zeros((W, slots), jnp.int32)], axis=0
    )
    pad_cnt = jnp.concatenate(
        [jnp.zeros((W,), jnp.int32), counts, jnp.zeros((W,), jnp.int32)], axis=0
    )
    sections = lax.axis_size("section")
    share = panels // sections
    start = first_panel + lax.axis_index("section") * share
    sliced = extended(tiles, (("col", 0),), W)
    windows = jnp.stack([sliced[t * share : t * share + share + 2 * W] for t in range(sections)], 0)
    whole = lax.all_to_all(windows, "section", split_axis=0, concat_axis=3, tiled=True)[0]
    win_off = lax.dynamic_slice_in_dim(pad_off, start, share + 2 * W, 0)
    win_cnt = lax.dynamic_slice_in_dim(pad_cnt, start, share + 2 * W, 0)
    loc_off = lax.dynamic_slice_in_dim(offsets, start, share, 0)
    loc_cnt = lax.dynamic_slice_in_dim(counts, start, share, 0)

    def one_whole(packed):
        p_off, p_cnt, centre = packed
        own = lax.dynamic_index_in_dim(whole, centre + W, 0, False)
        return expand(
            own, p_off, p_cnt, centre, start + centre, whole, win_off, win_cnt, total, bands
        )

    expanded = lax.map(one_whole, (loc_off, loc_cnt, jnp.arange(share, dtype=jnp.int32)))
    back = exchange_in_pieces(expanded, "section", 2, 2, 0)

    def one_finish(packed):
        values, rank_block = packed
        return finish(values, rank_block)

    return lax.map(one_finish, (back, ranks))


def solution(mesh):
    placed = (P("col", None, "section", None), P(), P(), P("col", None, "section", None))
    return jax.shard_map(
        shards,
        mesh=mesh,
        in_specs=placed,
        out_specs=P("col", None, "section", None),
        check_vma=False,
    )
```

profile of v0, /device:TPU:1, one launch (start us, length us, event | category | flops | bytes accessed | tf_op | source)
XLA Modules:
  0.0 636.4 jit_solution(12305052271781320024)
XLA Ops:
  19.8 8.3 %all-to-all-start = ((bf16[8,16,12,16,128]{4,3,2,1,0:T(8,128)(2,1)}), bf16[8,16,12,16,128]{4,3,2,1,0:T(8,128)(2,1)}, u32[]{:S(2)}, u32[]{:S(2)}) async-start(bf16[8,16,12,16,128]{4,3,2,1,0:T(8,128)(2,1)} %fusion.11), calls=%async_computation | async-start | bytes 12582912 | tf_op jit(solution)/shard_map/all_to_all | solution.py:94
  28.8 138.4 %all-to-all-done = bf16[8,16,12,16,128]{4,3,2,1,0:T(8,128)(2,1)} async-done(((bf16[8,16,12,16,128]{4,3,2,1,0:T(8,128)(2,1)}), bf16[8,16,12,16,128]{4,3,2,1,0:T(8,128)(2,1)}, u32[]{:S(2)}, u32[]{:S(2)}) %all-to-all-start) | async-done | bytes 6291488 | tf_op jit(solution)/shard_map/all_to_all | solution.py:94
  167.2 7.3 %copy.20 = bf16[1,16,12,8,16,128]{5,4,3,2,1,0:T(8,128)(2,1)} copy(bf16[1,16,12,8,16,128]{5,4,2,1,3,0:T(8,128)(2,1)} %bitcast.21) | data formatting | bytes 12582912 | tf_op jit(solution)/shard_map/all_to_all | solution.py:94
  174.5 199.5 %while.22 = (s32[]{:T(128)}, f32[4,25,128,128]{3,2,1,0:T(8,128)}, s32[4,12]{1,0:T(4,128)S(1)}, s32[4]{0:T(128)S(1)}, s32[16,12]{1,0:T(8,128)S(1)}, /*index=5*/bf...) while((s32[]{:T(128)}, f32[4,25,128,128]{3,2,1,0:T(8,128)}, ...), condition=%wide.region_2.3_spmd, body=%wide.region_0.2_spmd.sunk | while | flops 608701376 | bytes 76102056 | solution.py:107
  179.5 6.3 gather_fusion.2
  185.8 8.0 %broadcast_multiply_fusion.2 = f32[12,12,128,128]{3,2,1,0:T(8,128)} fusion(f32[12,12]{1,0:T(8,128)S(1)} %fusion.27, bf16[12,12,128,128]{3,2,1,0:T(8,128)(2,1)} %gather_fusion.2, bf16[16,12,128,128]{3,2,1,0:T(8,128)(2,1)} %get-tuple-element.310, s32[]{:T(128)S(6)} %select_n.67), kind=kOutput, calls=%fused_computation.10.clone.1 | convolution fusion | flops 606339072 | bytes 14549572 | tf_op jit(solution)/shard_map/while/body/eval_jaxpr/kcx,klxr->klcr/dot_general | solution.py:62
  193.9 9.6 %copy.29 = f32[144,128,128]{2,1,0:T(8,128)} copy(f32[144,128,128]{1,2,0:T(8,128)} %bitcast.73) | data formatting | bytes 18874368 | tf_op jit(solution)/shard_map/while/body/eval_jaxpr/reshape | solution.py:67
  203.9 19.1 %scatter_fusion = f32[25,128,128]{2,1,0:T(8,128)S(1)} fusion(f32[25,128,128]{2,1,0:T(8,128)S(1)} %broadcast.274, s32[144]{0:T(256)S(1)} %bitcast.79, f32[144,128,128]{2,1,0:T(8,128)} %copy.29), kind=kCustom, calls=%fused_computation.3.clone.1 | custom fusion | flops 2359296 | bytes 28312128 | tf_op jit(solution)/shard_map/while/body/eval_jaxpr/scatter-add | solution.py:67
  229.4 6.3 gather_fusion.2
  235.7 8.0 %broadcast_multiply_fusion.2 = f32[12,12,128,128]{3,2,1,0:T(8,128)} fusion(f32[12,12]{1,0:T(8,128)S(1)} %fusion.27, bf16[12,12,128,128]{3,2,1,0:T(8,128)(2,1)} %gather_fusion.2, bf16[16,12,128,128]{3,2,1,0:T(8,128)(2,1)} %get-tuple-element.310, s32[]{:T(128)S(6)} %select_n.67), kind=kOutput, calls=%fused_computation.10.clone.1 | convolution fusion | flops 606339072 | bytes 14549572 | tf_op jit(solution)/shard_map/while/body/eval_jaxpr/kcx,klxr->klcr/dot_general | solution.py:62
  243.7 9.6 %copy.29 = f32[144,128,128]{2,1,0:T(8,128)} copy(f32[144,128,128]{1,2,0:T(8,128)} %bitcast.73) | data formatting | bytes 18874368 | tf_op jit(solution)/shard_map/while/body/eval_jaxpr/reshape | solution.py:67
  253.8 19.1 %scatter_fusion = f32[25,128,128]{2,1,0:T(8,128)S(1)} fusion(f32[25,128,128]{2,1,0:T(8,128)S(1)} %broadcast.274, s32[144]{0:T(256)S(1)} %bitcast.79, f32[144,128,128]{2,1,0:T(8,128)} %copy.29), kind=kCustom, calls=%fused_computation.3.clone.1 | custom fusion | flops 2359296 | bytes 28312128 | tf_op jit(solution)/shard_map/while/body/eval_jaxpr/scatter-add | solution.py:67
  279.2 6.3 gather_fusion.2
  285.5 8.0 %broadcast_multiply_fusion.2 = f32[12,12,128,128]{3,2,1,0:T(8,128)} fusion(f32[12,12]{1,0:T(8,128)S(1)} %fusion.27, bf16[12,12,128,128]{3,2,1,0:T(8,128)(2,1)} %gather_fusion.2, bf16[16,12,128,128]{3,2,1,0:T(8,128)(2,1)} %get-tuple-element.310, s32[]{:T(128)S(6)} %select_n.67), kind=kOutput, calls=%fused_computation.10.clone.1 | convolution fusion | flops 606339072 | bytes 14549572 | tf_op jit(solution)/shard_map/while/body/eval_jaxpr/kcx,klxr->klcr/dot_general | solution.py:62
  293.6 9.6 %copy.29 = f32[144,128,128]{2,1,0:T(8,128)} copy(f32[144,128,128]{1,2,0:T(8,128)} %bitcast.73) | data formatting | bytes 18874368 | tf_op jit(solution)/shard_map/while/body/eval_jaxpr/reshape | solution.py:67
  303.6 19.1 %scatter_fusion = f32[25,128,128]{2,1,0:T(8,128)S(1)} fusion(f32[25,128,128]{2,1,0:T(8,128)S(1)} %broadcast.274, s32[144]{0:T(256)S(1)} %bitcast.79, f32[144,128,128]{2,1,0:T(8,128)} %copy.29), kind=kCustom, calls=%fused_computation.3.clone.1 | custom fusion | flops 2359296 | bytes 28312128 | tf_op jit(solution)/shard_map/while/body/eval_jaxpr/scatter-add | solution.py:67
  329.1 6.3 gather_fusion.2
  335.4 8.0 %broadcast_multiply_fusion.2 = f32[12,12,128,128]{3,2,1,0:T(8,128)} fusion(f32[12,12]{1,0:T(8,128)S(1)} %fusion.27, bf16[12,12,128,128]{3,2,1,0:T(8,128)(2,1)} %gather_fusion.2, bf16[16,12,128,128]{3,2,1,0:T(8,128)(2,1)} %get-tuple-element.310, s32[]{:T(128)S(6)} %select_n.67), kind=kOutput, calls=%fused_computation.10.clone.1 | convolution fusion | flops 606339072 | bytes 14549572 | tf_op jit(solution)/shard_map/while/body/eval_jaxpr/kcx,klxr->klcr/dot_general | solution.py:62
  343.4 9.6 %copy.29 = f32[144,128,128]{2,1,0:T(8,128)} copy(f32[144,128,128]{1,2,0:T(8,128)} %bitcast.73) | data formatting | bytes 18874368 | tf_op jit(solution)/shard_map/while/body/eval_jaxpr/reshape | solution.py:67
  353.4 19.1 %scatter_fusion = f32[25,128,128]{2,1,0:T(8,128)S(1)} fusion(f32[25,128,128]{2,1,0:T(8,128)S(1)} %broadcast.274, s32[144]{0:T(256)S(1)} %bitcast.79, f32[144,128,128]{2,1,0:T(8,128)} %copy.29), kind=kCustom, calls=%fused_computation.3.clone.1 | custom fusion | flops 2359296 | bytes 28312128 | tf_op jit(solution)/shard_map/while/body/eval_jaxpr/scatter-add | solution.py:67
  390.1 43.4 %all-to-all-done.1 = f32[8,4,8,16,128]{4,3,2,1,0:T(8,128)S(1)} async-done(((f32[8,4,8,16,128]{4,3,2,1,0:T(8,128)}), f32[8,4,8,16,128]{4,3,2,1,0:T(8,128)S(1)}, u32[]{:S(2)}, u32[]{:S(2)}) %all-to-all-start.1) | async-done | bytes 2097184 | tf_op jit(solution)/shard_map/all_to_all | solution.py:45
  438.4 98.0 %all-to-all-done.2 = f32[8,4,17,16,128]{4,3,2,1,0:T(8,128)} async-done(((f32[8,4,17,16,128]{4,3,2,1,0:T(8,128)}), f32[8,4,17,16,128]{4,3,2,1,0:T(8,128)}, u32[]{:S(2)}, u32[]{:S(2)}) %all-to-all-start.2) | async-done | bytes 4456480 | tf_op jit(solution)/shard_map/all_to_all | solution.py:45
  536.4 5.6 pad_maximum_fusion
  542.0 94.4 %while.23 = (s32[]{:T(128)}, bf16[32,25,16,128]{3,2,1,0:T(8,128)(2,1)}, s32[32,25,16,128]{3,2,1,0:T(8,128)}, f32[32,25,16,128]{3,2,1,0:T(8,128)}, s32[]{:T(128)}) while((s32[]{:T(128)}, bf16[32,25,16,128]{3,2,1,0:T(8,128)(2,1)}, s32[32,25,16,128]{3,2,1,0:T(8,128)}, f32[32,25,16,128]{3,2,1,0:T(8,128)}, s32[]{:T(128)}) %tuple.56), condition=%wide.region_5.6_spmd, body=%wide.region_3.5_spmd.sunk | while | flops 512002 | bytes 922433 | solution.py:114
  (194 shorter events, 155.0 us)
Async XLA Ops:
  0.0 13.4 %copy-start.1 = (bf16[32,12,16,128]{3,2,1,0:T(8,128)(2,1)S(1)}, bf16[32,12,16,128]{3,2,1,0:T(8,128)(2,1)}, u32[]{:S(2)}) copy-start(bf16[32,12,16,128]{3,2,1,0:T(8,128)(2,1)} %param.8) | copy-start | bytes 4718596
  1.3 8.2 %collective-permute-start = (bf16[6,12,16,128]{3,2,1,0:T(8,128)(2,1)S(1)}, bf16[6,12,16,128]{3,2,1,0:T(8,128)(2,1)S(1)}, u32[]{:S(2)}, u32[]{:S(2)}) collective-permute-start(bf16[6,12,16,128]{3,2,1,0:T(8,128)(2,1)S(1)} %get-tuple-element.184), channel_id=1, source_target_pairs={{0,1},{1,2},{2,3},{3,4},{4,5},{5,6},{6,7},{7,8},{8,9},{9,10},{10,1... | collective-permute-start | bytes 884744 | tf_op jit(solution)/shard_map/ppermute | solution.py:17
  5.8 11.9 %collective-permute-start.1 = (bf16[6,12,16,128]{3,2,1,0:T(8,128)(2,1)S(1)}, bf16[6,12,16,128]{3,2,1,0:T(8,128)(2,1)S(1)}, u32[]{:S(2)}, u32[]{:S(2)}) collective-permute-start(bf16[6,12,16,128]{3,2,1,0:T(8,128)(2,1)S(1)} %get-tuple-element.183), channel_id=1, source_target_pairs={{1,0},{2,1},{3,2},{4,3},{5,4},{6,5},{7,6},{8,7},{9,8},{10,9},{11,1... | collective-permute-start | bytes 884744 | tf_op jit(solution)/shard_map/ppermute | solution.py:18
  19.8 8.3 %copy-start.2 = (s32[1024,12]{0,1:T(8,128)S(1)}, s32[1024,12]{0,1:T(8,128)}, u32[]{:S(2)}) copy-start(s32[1024,12]{0,1:T(8,128)} %param.9) | copy-start | bytes 147460
  19.8 8.6 %copy-start.3 = (s32[1024]{0:T(1024)S(1)}, s32[1024]{0:T(1024)}, u32[]{:S(2)}) copy-start(s32[1024]{0:T(1024)} %param.10) | copy-start | bytes 12292
  19.8 147.4 %all-to-all-start = ((bf16[8,16,12,16,128]{4,3,2,1,0:T(8,128)(2,1)}), bf16[8,16,12,16,128]{4,3,2,1,0:T(8,128)(2,1)}, u32[]{:S(2)}, u32[]{:S(2)}) async-start(bf16[8,16,12,16,128]{4,3,2,1,0:T(8,128)(2,1)} %fusion.11), calls=%async_computation | async-start | bytes 12582912 | tf_op jit(solution)/shard_map/all_to_all | solution.py:94
  377.5 2.7 copy-start
  381.7 51.8 %all-to-all-start.1 = ((f32[8,4,8,16,128]{4,3,2,1,0:T(8,128)}), f32[8,4,8,16,128]{4,3,2,1,0:T(8,128)S(1)}, u32[]{:S(2)}, u32[]{:S(2)}) async-start(f32[8,4,8,16,128]{4,3,2,1,0:T(8,128)} %split.8), calls=%async_computation.1 | async-start | bytes 4194304 | tf_op jit(solution)/shard_map/all_to_all | solution.py:45
  433.6 102.8 %all-to-all-start.2 = ((f32[8,4,17,16,128]{4,3,2,1,0:T(8,128)}), f32[8,4,17,16,128]{4,3,2,1,0:T(8,128)}, u32[]{:S(2)}, u32[]{:S(2)}) async-start(f32[8,4,17,16,128]{4,3,2,1,0:T(8,128)} %split.9), calls=%async_computation.2 | async-start | bytes 8912896 | tf_op jit(solution)/shard_map/all_to_all | solution.py:45
where the time goes:
time: 647 us; the launch traced here: 636 us
  waiting for transfers between devices  282 us (44%)
  other arithmetic  179 us (28%)
  local copies, waits for them, and re-layouts  112 us (17%)
  matrix products  32.2 us (5%)
  starting transfers between devices  23.1 us (4%)
  loops' own time  8.03 us (1%)
    all_to_all x2, waiting for transfers between devices, exchange_in_pieces(): lax.all_to_all(share, axis, split_axis=0, concat_axis=0, tiled=True)  141 us
    all_to_all x1, waiting for transfers between devices, shards(): lax.all_to_all(windows, 'section', split_axis=0, concat_axis=3, tiled=True)  138 us
    scatter-add x4, other arithmetic, expand(): empty.at[target.reshape(-1)]  76.5 us
    dynamic_update_slice x32, other arithmetic, shards(): return lax.map(one_finish, (back, ranks))  56.6 us
    reshape x4, local copies, waits for them, and re-layouts, expand(): weighted.reshape((slots * slots, columns, rows))  38.3 us
    reduce_sum x32, other arithmetic, finish(): totals = jnp.sum(squared, axis=(0, 2), keepdims=True)  37.5 us
    dot_general x4, matrix products, expand(): jnp.einsum('kcx,klxr->klcr', own, firsts, preferred_element_type=jnp.floa...  32.2 us
    gather x4, local copies, waits for them, and re-layouts, expand(): firsts = banded[where_at]  25.3 us
  transfers between devices with their start and end apart: 5, of which 4 were waited for; matrix products, arithmetic and copies ran while one was open for 2% of the time, Pallas kernels for 0%

commit v1 on v0

v1 whole, which is shorter than its diff:
```python
import functools

import jax
import jax.numpy as jnp
from jax import lax
from jax.experimental import pallas as pl
from jax.experimental.pallas import tpu as pltpu
from jax.sharding import PartitionSpec as P

W = 6
TOPK = 256
GROUP = 4
MESH = pl.DeviceIdType.MESH


def list_rank(panels):
    return [m if m < W else (m - panels + 2 * W if m >= panels - W else m + W) for m in range(panels)]


def pack_kernel(panels, slots, first_ref, tiles_ref, out_ref):
    out_ref[...] = jnp.zeros_like(out_ref)
    order = sorted(range(panels), key=lambda m: list_rank(panels)[m])
    for m in order:
        at = first_ref[m]
        out_ref[pl.ds(at, slots)] = tiles_ref[m]


def cuts(start, stop, most):
    count = -(-(stop - start) // most)
    ends = [start + (stop - start) * i // count for i in range(count + 1)]
    return [(a, b - a) for a, b in zip(ends[:-1], ends[1:])]


def gather_kernel(n, m, edge, pieces, own_ref, g_ref, hl_ref, hr_ref, zs, zr, xs, xr, local_sem):
    s = lax.axis_index("section")
    c = lax.axis_index("col")
    ring = ({"section": lax.rem(s + 1, n)}, {"section": lax.rem(s + n - 1, n)})
    sides = ({"col": lax.rem(c + 1, m)}, {"col": lax.rem(c + m - 1, m)})
    halo = (hl_ref, hr_ref)
    half = n // 2

    barrier = pltpu.get_barrier_semaphore()
    for who in (*ring, *sides):
        pl.semaphore_signal(barrier, inc=1, device_id=who, device_id_type=MESH)
    pl.semaphore_wait(barrier, 4)

    def shard(way, hop):
        return lax.rem(s + (n - hop if way == 0 else hop), n)

    def source(way, hop, q):
        at, size = pieces[q]
        if hop == 0:
            return own_ref.at[pl.ds(at, size)]
        return g_ref.at[shard(way, hop), pl.ds(at, size)]

    def along(way, hop, q):
        at, size = pieces[q]
        return pltpu.make_async_remote_copy(
            src_ref=source(way, hop, q),
            dst_ref=g_ref.at[shard(way, hop), pl.ds(at, size)],
            send_sem=zs.at[way, hop, q],
            recv_sem=zr.at[way, hop, q],
            device_id=ring[way],
            device_id_type=MESH,
        )

    def across(side, way, hop, q):
        at, size = pieces[q]
        turn = n - 1 if hop == half else hop if way == 0 else half - 1 + hop
        return pltpu.make_async_remote_copy(
            src_ref=source(way, hop, q),
            dst_ref=halo[side].at[shard(way, hop), pl.ds(at, size)],
            send_sem=xs.at[side, turn, q],
            recv_sem=xr.at[side, turn, q],
            device_id=sides[side],
            device_id_type=MESH,
        )

    def travels(way, hop, q):
        return hop < half - 1 or q % 2 == way

    count = len(pieces)
    sent, crossed = [], []
    keep = pltpu.make_async_copy(own_ref.at[pl.ds(0, g_ref.shape[1])], g_ref.at[s], local_sem)
    for hop in range(half + 1):
        for q in range(count):
            for way in (0, 1):
                if hop > 0:
                    if not travels(way, hop - 1, q):
                        continue
                    along(way, hop - 1, q).wait_recv()
                if hop < half and travels(way, hop, q):
                    copy = along(way, hop, q)
                    copy.start()
                    sent.append(copy)
                if pieces[q][0] < edge and (hop > 0 or way == 0):
                    for side in (0, 1):
                        copy = across(side, way, hop, q)
                        copy.start()
                        crossed.append(copy)
        if hop == 0:
            keep.start()
    keep.wait()
    for copy in crossed:
        copy.wait_recv()
    for copy in crossed + sent:
        copy.wait_send()


def expand_kernel(
    n, share, edge, wide, slots, bands, tab_ref, own_ref, g_ref, hl_ref, hr_ref, ranks_ref, out_ref, v_ref, lhs_ref, acc_ref, sems
):
    step = pl.program_id(0)
    s = lax.axis_index("section")
    offs = 2 * W + 1
    across = GROUP + 2 * W
    zero_at = wide + 2 * edge

    @pl.when(step == 0)
    def load():
        copies = [
            pltpu.make_async_copy(g_ref, v_ref.at[:, pl.ds(0, wide)], sems.at[0]),
            pltpu.make_async_copy(hl_ref, v_ref.at[:, pl.ds(wide, edge)], sems.at[1]),
            pltpu.make_async_copy(hr_ref, v_ref.at[:, pl.ds(wide + edge, edge)], sems.at[2]),
        ]
        for copy in copies:
            copy.start()
        v_ref[:, zero_at] = jnp.zeros_like(v_ref[:, zero_at])
        acc_ref[...] = jnp.zeros_like(acc_ref)
        for copy in copies:
            copy.wait()

    tile = n * share
    none = jnp.zeros((tile, tile), v_ref.dtype)
    for a in range(across):
        for p in range(GROUP):
            d = p + W - a
            if abs(d) > W:
                block = jnp.zeros((share, tile), v_ref.dtype)
            else:
                block = v_ref[s, own_ref[(step * GROUP + a) * offs + d + W]]
            lhs_ref[a * share : (a + 1) * share, p * tile : (p + 1) * tile] = block

    def slot(a):
        return lax.rem(step * GROUP + a, across)

    for pair in range(across // 2):
        cols = []
        for b in (2 * pair, 2 * pair + 1):
            rows = []
            for p in range(GROUP):
                e = b - W - p
                if abs(e) > W:
                    rows.append(none)
                else:
                    got = v_ref[:, tab_ref[(step * GROUP + p) * offs + e + W]]
                    rows.append(got.reshape(tile, tile))
            cols.append(jnp.concatenate(rows, axis=0))
        rhs = jnp.concatenate(cols, axis=1)
        res = jnp.dot(lhs_ref[...], rhs, preferred_element_type=jnp.float32)
        for i in (0, 1):
            b = 2 * pair + i
            for a in range(across):
                o = b - a + 2 * W
                if 0 <= o < bands:
                    acc_ref[slot(a), o] += res[a * share : (a + 1) * share, i * tile : (i + 1) * tile]

    @pl.when(step >= 2 * W // GROUP)
    def finish():
        for a in range(GROUP):
            at = slot(a)
            value = acc_ref[at]
            squared = jnp.where(ranks_ref[a] < TOPK, value * value, jnp.float32(0.0))
            totals = jnp.sum(jnp.sum(squared, axis=0), axis=1, keepdims=True)
            out_ref[a] = (squared * (TOPK / (totals + 1e-6))[None]).astype(out_ref.dtype)

    for a in range(GROUP):
        acc_ref[slot(a)] = jnp.zeros(acc_ref.shape[1:], acc_ref.dtype)


def shards(tiles, offsets, counts, ranks):
    panels, slots, share, tile = tiles.shape
    bands = ranks.shape[1]
    total = offsets.shape[0]
    n = lax.axis_size("section")
    m = lax.axis_size("col")
    offs = 2 * W + 1
    edge = 2 * W * slots
    full = panels * slots
    col = lax.axis_index("col")
    first = col * panels

    rank_of = jnp.array(list_rank(panels), jnp.int32)
    before = (rank_of[:, None] < rank_of[None, :]).astype(jnp.float32)
    by_col = counts.reshape(m, panels).astype(jnp.float32)
    starts = jnp.dot(by_col, before, preferred_element_type=jnp.float32).astype(jnp.int32)
    most = jnp.max(jnp.sum(counts.reshape(m, panels), axis=1))

    packed = pl.pallas_call(
        functools.partial(pack_kernel, panels, slots),
        out_shape=jax.ShapeDtypeStruct((full + slots, share, tile), tiles.dtype),
        in_specs=[pl.BlockSpec(memory_space=pltpu.SMEM), pl.BlockSpec(memory_space=pltpu.VMEM)],
        out_specs=pl.BlockSpec(memory_space=pltpu.VMEM),
        name="pack",
    )(lax.dynamic_index_in_dim(starts, col, 0, False), tiles)

    reach = panels + 2 * W
    where = first - 3 * W + W + jnp.arange(reach, dtype=jnp.int32) + W
    at = jnp.clip(where, 0, total - 1)
    win_off = offsets[at]
    win_cnt = jnp.where((where >= 0) & (where < total), counts[at], 0)
    win_start = starts.reshape(total)[at]
    ids = jnp.arange(slots, dtype=jnp.int32)
    rows = where[:, None] + win_off
    ok = (ids[None] < win_cnt[:, None]) & (rows >= 0) & (rows < total)
    hit = ok[:, None, :] & (win_off[:, None, :] == jnp.arange(-W, W + 1, dtype=jnp.int32)[None, :, None])
    found = jnp.sum(jnp.where(hit, ids[None, None] + 1, 0), axis=2)

    def level(wide):
        pieces = cuts(0, edge, 48) + cuts(edge, wide, 64)
        count = len(pieces)
        edges = sum(1 for at, _ in pieces if at < edge)

        def run(packed, found, win_start, ranks):
            base = jnp.where(where < first, wide, jnp.where(where < first + panels, 0, wide + edge))
            none = wide + 2 * edge
            tab = jnp.where(found > 0, (base + win_start)[:, None] + found - 1, none)
            mine = jnp.full((panels + 4 * W, offs), none, jnp.int32)
            mine = lax.dynamic_update_slice(mine, tab[W : W + panels], (2 * W, 0))
            g, hl, hr = pl.pallas_call(
                functools.partial(gather_kernel, n, m, edge, pieces),
                out_shape=(
                    jax.ShapeDtypeStruct((n, wide, share, tile), tiles.dtype),
                    jax.ShapeDtypeStruct((n, edge, share, tile), tiles.dtype),
                    jax.ShapeDtypeStruct((n, edge, share, tile), tiles.dtype),
                ),
                in_specs=[pl.BlockSpec(memory_space=pltpu.VMEM)],
                out_specs=(pl.BlockSpec(memory_space=pl.ANY),) * 3,
                scratch_shapes=[
                    pltpu.SemaphoreType.DMA((2, n // 2, count)),
                    pltpu.SemaphoreType.DMA((2, n // 2, count)),
                    pltpu.SemaphoreType.DMA((2, n, edges)),
                    pltpu.SemaphoreType.DMA((2, n, edges)),
                    pltpu.SemaphoreType.DMA,
                ],
                compiler_params=pltpu.CompilerParams(collective_id=wide // 16, has_side_effects=True),
                name=f"gather{wide}",
            )(packed)
            steps = reach // GROUP
            lag = 2 * W // GROUP
            block = pl.BlockSpec((GROUP, bands, share, tile), lambda i, *_: (jnp.maximum(i - lag, 0), 0, 0, 0))
            return pl.pallas_call(
                functools.partial(expand_kernel, n, share, edge, wide, slots, bands),
                out_shape=jax.ShapeDtypeStruct(ranks.shape, jnp.bfloat16),
                grid_spec=pltpu.PrefetchScalarGridSpec(
                    num_scalar_prefetch=2,
                    grid=(steps,),
                    in_specs=[pl.BlockSpec(memory_space=pl.ANY)] * 3 + [block],
                    out_specs=block,
                    scratch_shapes=[
                        pltpu.VMEM((n, wide + 2 * edge + 1, share, tile), tiles.dtype),
                        pltpu.VMEM(((GROUP + 2 * W) * share, GROUP * tile), tiles.dtype),
                        pltpu.VMEM((GROUP + 2 * W, bands, share, tile), jnp.float32),
                        pltpu.SemaphoreType.DMA((3,)),
                    ],
                ),
                compiler_params=pltpu.CompilerParams(vmem_limit_bytes=60 * 1024 * 1024),
                name=f"expand{wide}",
            )(tab.reshape(-1), mine.reshape(-1), g, hl, hr, ranks)

        return run

    wides = [full * i // 12 for i in (6, 7, 8, 9, 12)]
    pick = sum((most > wide).astype(jnp.int32) for wide in wides[:-1])
    return lax.switch(pick, [level(wide) for wide in wides], packed, found, win_start, ranks)


def solution(mesh):
    placed = (P("col", None, "section", None), P(), P(), P("col", None, "section", None))
    return jax.shard_map(
        shards,
        mesh=mesh,
        in_specs=placed,
        out_specs=P("col", None, "section", None),
        check_vma=False,
    )
```

time: 647 us -> 136 us (0.21); the launches traced: 636 us -> 134 us
  waiting for transfers between devices: 282 us -> 0 us
  other arithmetic: 179 us -> 0.99 us
  Pallas kernels: 0 us -> 121 us
  local copies, waits for them, and re-layouts: 112 us -> 8.84 us
  matrix products: 32.2 us -> 0.93 us
  starting transfers between devices: 23.1 us -> 0 us
  loops' own time: 8.03 us -> 0.31 us
    all_to_all x3 -> x0, waiting for transfers between devices: 280 us -> none  [the longest x2 141 us: exchange_in_pieces(): lax.all_to_all(share, axis, split_axis=0, concat_axis=0, tiled=True)]
    pallas_call x0 -> x3, Pallas kernels: none -> 121 us  [the longest x1 92.6 us: run(): pl.pallas_call(functools.partial(gather_kernel, n, m, edge, pieces), out_...]
    scatter-add x4 -> x0, other arithmetic: 76.5 us -> none  [expand(): empty.at[target.reshape(-1)]]
    dynamic_update_slice x32 -> x0, other arithmetic: 56.6 us -> none  [shards(): return lax.map(one_finish, (back, ranks))]
    reshape x5 -> x4, local copies, waits for them, and re-layouts: 41.8 us -> 2.26 us  [the longest x1 0.76 us: shards(): most = jnp.max(jnp.sum(counts.reshape(m, panels), axis=1))]
    reduce_sum x32 -> x2, other arithmetic: 37.5 us -> 0.21 us  [the longest x1 0.12 us: shards(): most = jnp.max(jnp.sum(counts.reshape(m, panels), axis=1))]
    dot_general x4 -> x1, matrix products: 32.2 us -> 0.93 us  [shards(): jnp.dot(by_col, before, preferred_element_type=jnp.float32)]
    gather x12 -> x3, local copies, waits for them, and re-layouts: 30.1 us -> 2.78 us  [the longest x1 1.46 us: shards(): win_cnt = jnp.where((where >= 0) & (where < total), counts[at], 0)]
  transfers between devices with their start and end apart: 5 -> 0, of which waited for: 4 -> 0; matrix products, arithmetic and copies ran while one was open for 2% -> 0% of each run, Pallas kernels for 0% -> 0%
where the time goes in v1:
time: 136 us; the launch traced here: 134 us
  Pallas kernels  121 us (89%)
  local copies, waits for them, and re-layouts  8.84 us (6%)
  between operations  2.68 us (2%)
    pallas_call x1, Pallas kernels, run(): pl.pallas_call(functools.partial(gather_kernel, n, m, edge, pieces), out_...  92.6 us
    pallas_call x1, Pallas kernels, run(): pl.pallas_call(functools.partial(expand_kernel, n, share, edge, wide, slo...  26.4 us
    unnamed x3, local copies, waits for them, and re-layouts  2.75 us

profile of v1, /device:TPU:1, one launch (start us, length us, event | category | flops | bytes accessed | tf_op | source)
XLA Modules:
  0.0 134.5 jit_solution(8432015953818899135)
XLA Ops:
  0.1 0.8 reshape.123
  0.8 0.1 reduce_sum.18
  0.9 0.6 reduce_max.9
  4.2 0.9 convolution_convert_fusion
  5.1 0.5 dynamic-slice_bitcast_fusion.first_ref
  5.6 1.0 copy.114
  6.7 0.6 gather_fusion.10
  7.3 0.1 broadcast_add_fusion.10
  7.3 1.7 %pack.1 = bf16[396,16,128]{2,1,0:T(8,128)(2,1)S(1)} custom-call(s32[32]{0:T(128)} %dynamic-slice_bitcast_fusion.first_ref, bf16[32,12,16,128]{3,2,1,0:T(8,128)(2,1)} %tiles_ref.1), custom_call_target="tpu_custom_call" | custom-call | tf_op jit(solution)/shard_map/pack/pallas_call | solution.py:199
  9.1 123.7 %conditional.1 = (bf16[32,25,16,128]{3,2,1,0:T(8,128)(2,1)S(1)}) conditional(s32[]{:T(128)} %clamp.11, (s32[44,12]{0,1:T(8,128)S(1)}, s32[]{:T(128)}, s32[44]{0:T(128)S(1)}, s32[32,32]{1,0:T(8,128)S(1)}, bf16[396,16,128]{2,1,0:T(8,128)(2,1)S(1)}, /*index=5*/s32[32,25,16,128]{3,2,1,0:T(8,128)}, s32[]{:T(128)}, ...), branch_computations={%region_3.4_spmd.clone, %region_4.5_spmd.clone, %region_5.6_spmd.c... | conditional | flops 33258 | bytes 70880 | solution.py:275
  9.2 1.5 %gather_fusion.5 = s32[44]{0:T(128)S(1)} fusion(s32[1024]{0:T(1024)} %get-tuple-element.481, s32[1024]{0:T(1024)S(1)} %pad_clamp_fusion.2), kind=kCustom, calls=%fused_computation.5 | custom fusion | bytes 528 | tf_op jit(solution)/shard_map/gather | solution.py:211
  10.7 0.7 gather_fusion.4
  11.4 0.1 copy.123
  11.5 0.1 copy.122
  11.6 0.1 copy.121
  11.7 0.1 select_reduce_fusion.2
  11.8 0.1 slice.44
  11.9 0.1 copy.132
  12.0 0.7 reshape.137.own_ref
  12.7 0.1 copy.108
  12.8 0.7 reshape.136.tab_ref
  13.5 92.6 %gather256.1 = (bf16[8,256,16,128]{3,2,1,0:T(8,128)(2,1)}, bf16[8,144,16,128]{3,2,1,0:T(8,128)(2,1)}, bf16[8,144,16,128]{3,2,1,0:T(8,128)(2,1)}) custom-call(bf16[396,16,128]{2,1,0:T(8,128)(2,1)S(1)} %get-tuple-element.463.own_ref), custom_call_target="tpu_custom_call" | custom-call | tf_op jit(solution)/shard_map/cond/branch_2_fun/gather256/pallas_call | solution.py:230
  106.1 26.4 %expand256.1 = bf16[32,25,16,128]{3,2,1,0:T(8,128)(2,1)S(1)} custom-call(s32[572]{0:T(1024)} %reshape.136.tab_ref, s32[728]{0:T(1024)} %reshape.137.own_ref, bf16[8,256,16,128]{3,2,1,0:T(8,128)(2,1)} %get-tuple-element.464.g_ref, bf16[8,144,16,128]{3,2,1,0:T(8,128)(2,1)} %get-tuple-element.465.hl_ref, bf16[8,144,16,128]{3,2,1,0:T(8,128)(2,1)} %get-tuple-element.466.hr_ref, ...), custom_call_target="tpu_custom_call" | custom-call | tf_op jit(solution)/shard_map/cond/branch_2_fun/expand256/pallas_call | solution.py:252
  132.8 1.7 %copy-done = bf16[32,25,16,128]{3,2,1,0:T(8,128)(2,1)} copy-done((bf16[32,25,16,128]{3,2,1,0:T(8,128)(2,1)}, bf16[32,25,16,128]{3,2,1,0:T(8,128)(2,1)S(1)}, u32[]{:S(2)}) %copy-start) | copy-done | bytes 3276824
  (17 shorter events, 0.2 us)
Async XLA Ops:
  132.8 1.7 %copy-start = (bf16[32,25,16,128]{3,2,1,0:T(8,128)(2,1)}, bf16[32,25,16,128]{3,2,1,0:T(8,128)(2,1)S(1)}, u32[]{:S(2)}) copy-start(bf16[32,25,16,128]{3,2,1,0:T(8,128)(2,1)S(1)} %get-tuple-element.1037) | copy-start | bytes 9830404

commit v2 on v1

v2 whole, which is shorter than its diff:
```python
import functools

import jax
import jax.numpy as jnp
from jax import lax
from jax.experimental import pallas as pl
from jax.experimental.pallas import tpu as pltpu
from jax.sharding import PartitionSpec as P

W = 6
TOPK = 256
GROUP = 8
STRIDE = 16
WIDES = (192, 224, 240, 256, 272, 288, 320)
MESH = pl.DeviceIdType.MESH


def plan_kernel(m, wides, edge, counts_ref, offsets_ref, lanes_ref, tiles_ref, packed_ref, tab_ref, pick_ref):
    panels, slots = tiles_ref.shape[:2]
    col = lax.axis_index("col")
    none = 2 * edge
    base = none + 1

    def run(row, count, owner, begin, at, region, pack):
        valid = (owner >= 0) & (owner < m)
        lead = jnp.clip(owner, 0, m - 1) * panels + begin

        def panel(i, at):
            p = lead + i
            used = jnp.where(valid, counts_ref[p], 0)
            line = (row + i) * STRIDE + W
            place = region + at
            left = line
            for k in range(slots):
                off = offsets_ref[k, p]
                tab_ref[line + off] = jnp.where(k < used, place + k, none)
                left = left - off
            tab_ref[left] = none
            if pack:
                packed_ref[pl.ds(at, slots)] = tiles_ref[begin + i]
            return at + used

        return lax.fori_loop(0, count, panel, at)

    at = run(W, W, col, 0, 0, base, True)
    at = run(panels, W, col, panels - W, at, base, True)
    run(2 * W, panels - 2 * W, col, W, at, base, True)
    lead = jnp.maximum(col - 1, 0) * panels
    ahead = counts_ref[lead]
    for i in range(1, W):
        ahead = ahead + counts_ref[lead + i]
    run(0, W, col - 1, panels - W, ahead, 0, False)
    run(W + panels, W, col + 1, 0, 0, edge, False)

    @pl.when(col == 0)
    def top():
        for i in range(W):
            for e in range(W - i):
                tab_ref[(W + i) * STRIDE + e] = none

    @pl.when(col == m - 1)
    def bottom():
        for i in range(W):
            for e in range(W - i):
                tab_ref[(W + panels - 1 - i) * STRIDE + 2 * W - e] = none

    same = lax.broadcasted_iota(jnp.int32, (128, 128), 0) // panels == lax.broadcasted_iota(jnp.int32, (128, 128), 1) // panels
    sums = jnp.dot(
        lanes_ref[...].astype(jnp.float32).astype(jnp.bfloat16),
        same.astype(jnp.float32).astype(jnp.bfloat16),
        preferred_element_type=jnp.float32,
    )
    most = jnp.max(sums).astype(jnp.int32)
    pick = 0
    for wide in wides[:-1]:
        pick = pick + (most > wide).astype(jnp.int32)
    pick_ref[0] = pick


def cuts(start, stop, most):
    count = -(-(stop - start) // most)
    ends = [start + (stop - start) * i // count for i in range(count + 1)]
    return [(a, b - a) for a, b in zip(ends[:-1], ends[1:])]


def gather_kernel(n, m, edge, wide, pieces, own_ref, v_ref, zs, zr, xs, xr):
    s = lax.axis_index("section")
    c = lax.axis_index("col")
    ring = ({"section": lax.rem(s + 1, n)}, {"section": lax.rem(s + n - 1, n)})
    sides = ({"col": lax.rem(c + 1, m)}, {"col": lax.rem(c + m - 1, m)})
    zero_at = 2 * edge
    base = zero_at + 1
    half = n // 2

    barrier = pltpu.get_barrier_semaphore()
    for who in (*ring, *sides):
        pl.semaphore_signal(barrier, inc=1, device_id=who, device_id_type=MESH)
    pl.semaphore_wait(barrier, 4)

    def shard(way, hop):
        return lax.rem(s + (n - hop if way == 0 else hop), n)

    def source(way, hop, q):
        at, size = pieces[q]
        if hop == 0:
            return own_ref.at[pl.ds(at, size)]
        return v_ref.at[shard(way, hop), pl.ds(base + at, size)]

    def along(way, hop, q):
        at, size = pieces[q]
        return pltpu.make_async_remote_copy(
            src_ref=source(way, hop, q),
            dst_ref=v_ref.at[shard(way, hop), pl.ds(base + at, size)],
            send_sem=zs.at[way, hop, q],
            recv_sem=zr.at[way, hop, q],
            device_id=ring[way],
            device_id_type=MESH,
        )

    def across(side, way, hop, q):
        at, size = pieces[q]
        turn = n - 1 if hop == half else hop if way == 0 else half - 1 + hop
        return pltpu.make_async_remote_copy(
            src_ref=source(way, hop, q),
            dst_ref=v_ref.at[shard(way, hop), pl.ds(side * edge + at, size)],
            send_sem=xs.at[side, turn, q],
            recv_sem=xr.at[side, turn, q],
            device_id=sides[side],
            device_id_type=MESH,
        )

    def travels(way, hop, q):
        return hop < half - 1 or q % 2 == way

    count = len(pieces)
    sent, crossed = [], []
    for hop in range(half + 1):
        for q in range(count):
            for way in (0, 1):
                if hop > 0:
                    if not travels(way, hop - 1, q):
                        continue
                    along(way, hop - 1, q).wait_recv()
                if hop < half and travels(way, hop, q):
                    copy = along(way, hop, q)
                    copy.start()
                    sent.append(copy)
                if pieces[q][0] < edge and (hop > 0 or way == 0):
                    for side in (0, 1):
                        copy = across(side, way, hop, q)
                        copy.start()
                        crossed.append(copy)
        if hop == 0:
            v_ref[:, zero_at] = jnp.zeros_like(v_ref[:, zero_at])
            v_ref[s, pl.ds(base, wide)] = own_ref[pl.ds(0, wide)]
    for copy in crossed:
        copy.wait_recv()
    for copy in crossed + sent:
        copy.wait_send()


def expand_kernel(n, bands, tab_ref, v_ref, ranks_ref, out_ref, lhs_ref, sq_ref):
    step = pl.program_id(0)
    s = lax.axis_index("section")
    share, tile = v_ref.shape[2:]
    mids = GROUP + 2 * W
    ends = GROUP + 4 * W

    def where(p, e):
        return tab_ref[(step * GROUP + p) * STRIDE + e + W]

    for a in range(GROUP):
        for p in range(mids):
            d = p - W - a
            rows, cols = slice(a * share, (a + 1) * share), slice(p * tile, (p + 1) * tile)
            if abs(d) <= W:
                lhs_ref[rows, cols] = v_ref[s, where(a + W, d)]
            else:
                lhs_ref[rows, cols] = jnp.zeros((share, tile), lhs_ref.dtype)

    empty = jnp.zeros((tile, tile), v_ref.dtype)
    sums = [jnp.zeros((share, tile), jnp.float32) for _ in range(GROUP)]
    for b in range(0, ends, 2):
        lo, hi = max(0, b - 2 * W), min(mids, b + 2)
        sides = []
        for r in (b, b + 1):
            rows = []
            for p in range(lo, hi):
                e = r - W - p
                if abs(e) <= W:
                    rows.append(v_ref[:, where(p, e)].reshape(tile, tile))
                else:
                    rows.append(empty)
            sides.append(jnp.concatenate(rows, axis=0))
        res = jnp.dot(
            lhs_ref[:, lo * tile : hi * tile],
            jnp.concatenate(sides, axis=1),
            preferred_element_type=jnp.float32,
        )
        for i in (0, 1):
            for a in range(GROUP):
                o = b + i - a
                if 0 <= o < bands:
                    value = res[a * share : (a + 1) * share, i * tile : (i + 1) * tile]
                    squared = jnp.where(ranks_ref[step * GROUP + a, o] < TOPK, value * value, jnp.float32(0.0))
                    sq_ref[a, o] = squared
                    sums[a] = sums[a] + squared
    for a in range(GROUP):
        totals = jnp.sum(sums[a], axis=1, keepdims=True)
        out_ref[a] = (sq_ref[a] * (TOPK / (totals + 1e-6))[None]).astype(out_ref.dtype)


def shards(tiles, offsets, counts, ranks):
    panels, slots, share, tile = tiles.shape
    bands = ranks.shape[1]
    n = lax.axis_size("section")
    m = lax.axis_size("col")
    edge = 2 * W * slots
    full = panels * slots
    wides = [w for w in WIDES if edge < w < full] + [full]
    scalars = pl.BlockSpec(memory_space=pltpu.SMEM)
    near = pl.BlockSpec(memory_space=pltpu.VMEM)

    packed, tab, pick = pl.pallas_call(
        functools.partial(plan_kernel, m, wides, edge),
        out_shape=(
            jax.ShapeDtypeStruct((full + slots, share, tile), tiles.dtype),
            jax.ShapeDtypeStruct(((panels + 2 * W) * STRIDE,), jnp.int32),
            jax.ShapeDtypeStruct((1,), jnp.int32),
        ),
        in_specs=[scalars, scalars, near, near],
        out_specs=(near, scalars, scalars),
        compiler_params=pltpu.CompilerParams(vmem_limit_bytes=8 << 20),
        name="plan",
    )(counts, offsets.T, counts.reshape(-1, 128), tiles)

    def level(wide):
        pieces = cuts(0, edge, 48) + cuts(edge, wide, 64)
        count = len(pieces)
        edges = sum(1 for at, _ in pieces if at < edge)

        def run(packed, tab, ranks):
            v = pl.pallas_call(
                functools.partial(gather_kernel, n, m, edge, wide, pieces),
                out_shape=jax.ShapeDtypeStruct((n, 2 * edge + 1 + wide, share, tile), tiles.dtype),
                in_specs=[near],
                out_specs=near,
                scratch_shapes=[
                    pltpu.SemaphoreType.DMA((2, n // 2, count)),
                    pltpu.SemaphoreType.DMA((2, n // 2, count)),
                    pltpu.SemaphoreType.DMA((2, n, edges)),
                    pltpu.SemaphoreType.DMA((2, n, edges)),
                ],
                compiler_params=pltpu.CompilerParams(
                    collective_id=wide // 8, has_side_effects=True, vmem_limit_bytes=8 << 20
                ),
                name=f"gather{wide}",
            )(packed)
            block = pl.BlockSpec((GROUP, bands, share, tile), lambda i, *_: (i, 0, 0, 0))
            return pl.pallas_call(
                functools.partial(expand_kernel, n, bands),
                out_shape=pltpu.HBM(ranks.shape, jnp.bfloat16),
                grid_spec=pltpu.PrefetchScalarGridSpec(
                    num_scalar_prefetch=1,
                    grid=(panels // GROUP,),
                    in_specs=[near, near],
                    out_specs=block,
                    scratch_shapes=[
                        pltpu.VMEM((GROUP * share, (GROUP + 2 * W) * tile), tiles.dtype),
                        pltpu.VMEM((GROUP, bands, share, tile), jnp.float32),
                    ],
                ),
                compiler_params=pltpu.CompilerParams(vmem_limit_bytes=30 << 20),
                name=f"expand{wide}",
            )(tab, v, ranks)

        return run

    return lax.switch(pick[0], [level(wide) for wide in wides], packed, tab, ranks)


def solution(mesh):
    placed = (P("col", None, "section", None), P(), P(), P("col", None, "section", None))
    return jax.shard_map(
        shards,
        mesh=mesh,
        in_specs=placed,
        out_specs=P("col", None, "section", None),
        check_vma=False,
    )
```

time: 136 us -> 111 us (0.82)
  Pallas kernels: 121 us -> 106 us
  local copies, waits for them, and re-layouts: 8.84 us -> 2.94 us
  between operations: 2.68 us -> 0.66 us
    pallas_call x3, Pallas kernels: 121 us -> 106 us  [the longest x1 92.2 us: run(): pl.pallas_call(functools.partial(gather_kernel, n, m, edge, wide, pieces)...]
    gather x3 -> x0, local copies, waits for them, and re-layouts: 2.78 us -> none  [the longest x1 1.46 us: shards(): win_cnt = jnp.where((where >= 0) & (where < total), counts[at], 0)]
    reshape x4 -> x0, local copies, waits for them, and re-layouts: 2.26 us -> none  [the longest x1 0.76 us: shards(): most = jnp.max(jnp.sum(counts.reshape(m, panels), axis=1))]
    unnamed x3 -> x6, local copies, waits for them, and re-layouts: 2.75 us -> 2.93 us
where the time goes in v2:
time: 111 us; the launch traced here: 109 us
  Pallas kernels  106 us (95%)
  local copies, waits for them, and re-layouts  2.94 us (3%)
    pallas_call x1, Pallas kernels, run(): pl.pallas_call(functools.partial(gather_kernel, n, m, edge, wide, pieces)...  92.2 us
    pallas_call x1, Pallas kernels, run(): pl.pallas_call(functools.partial(expand_kernel, n, bands), out_shape=pltp...  9.14 us
    pallas_call x1, Pallas kernels, shards(): pl.pallas_call(functools.partial(plan_kernel, m, wides, edge), out_shape=...  4.4 us
    unnamed x6, local copies, waits for them, and re-layouts  2.93 us

profile of v2, /device:TPU:1, one launch (start us, length us, event | category | flops | bytes accessed | tf_op | source)
XLA Modules:
  0.0 109.4 jit_solution(7064091160095035841)
XLA Ops:
  0.0 0.0 copy-start
  0.0 1.4 %copy-done = bf16[32,12,16,128]{3,2,1,0:T(8,128)(2,1)S(1)} copy-done((bf16[32,12,16,128]{3,2,1,0:T(8,128)(2,1)S(1)}, bf16[32,12,16,128]{3,2,1,0:T(8,128)(2,1)}, u32[]{:S(2)}) %copy-start) | copy-done | bytes 1572888
  1.4 0.0 copy-start.1
  1.4 0.8 copy-done.1
  2.2 0.0 copy-start.2
  2.3 0.7 copy-done.2
  2.9 4.4 %plan.1 = (bf16[396,16,128]{2,1,0:T(8,128)(2,1)S(1)}, s32[704]{0:T(1024)S(1)}, s32[1]{0:T(128)}) custom-call(s32[1024]{0:T(1024)S(1)} %copy-done.2, s32[12,1024]{1,0:T(8,128)S(1)} %bitcast.3, s32[8,128]{1,0:T(8,128)S(1)} %bitcast.4, bf16[32,12,16,128]{3,2,1,0:T(8,128)(2,1)S(1)} %copy-done), custom_call_target="tpu_custom_call" | custom-call | tf_op jit(solution)/shard_map/plan/pallas_call | solution.py:224
  8.0 101.4 %conditional.1 = (bf16[32,25,16,128]{3,2,1,0:T(8,128)(2,1)}) conditional(s32[]{:T(128)} %bitcast.2, (bf16[396,16,128]{2,1,0:T(8,128)(2,1)S(1)}, s32[704]{0:T(1024)S(1)}, s32[32,25,16,128]{3,2,1,0:T(8,128)}) %tuple.29, (bf16[396,16,128]{2,1,0:T(8,128)(2,1)S(1)}, s32[704]{0:T(1024)S(1)}, ...), branch_computations={%region_0.0_spmd, %region_1.0_spmd, %region_2.0_spmd, %region_3.0_... | conditional | bytes 26214436 | solution.py:279
  8.0 0.0 copy-start.6
  8.0 92.2 %gather256.1.v_ref = bf16[8,545,16,128]{3,2,1,0:T(8,128)(2,1)S(1)} custom-call(bf16[396,16,128]{2,1,0:T(8,128)(2,1)S(1)} %get-tuple-element.72.own_ref), custom_call_target="tpu_custom_call" | custom-call | tf_op jit(solution)/shard_map/cond/branch_3_fun/gather256/pallas_call | solution.py:243
  100.2 0.0 copy-done.6
  100.3 9.1 %expand256.1 = bf16[32,25,16,128]{3,2,1,0:T(8,128)(2,1)} custom-call(s32[704]{0:T(1024)S(1)} %get-tuple-element.71.tab_ref, bf16[8,545,16,128]{3,2,1,0:T(8,128)(2,1)S(1)} %gather256.1.v_ref, s32[32,25,16,128]{3,2,1,0:T(8,128)S(1)} %copy-done.6), custom_call_target="tpu_custom_call" | custom-call | tf_op jit(solution)/shard_map/cond/branch_3_fun/expand256/pallas_call | solution.py:260
Async XLA Ops:
  0.0 1.4 %copy-start = (bf16[32,12,16,128]{3,2,1,0:T(8,128)(2,1)S(1)}, bf16[32,12,16,128]{3,2,1,0:T(8,128)(2,1)}, u32[]{:S(2)}) copy-start(bf16[32,12,16,128]{3,2,1,0:T(8,128)(2,1)} %tiles_ref.1) | copy-start | bytes 4718596
  1.4 0.8 copy-start.1
  2.2 0.7 copy-start.2
  8.0 92.2 %copy-start.6 = (s32[32,25,16,128]{3,2,1,0:T(8,128)S(1)}, s32[32,25,16,128]{3,2,1,0:T(8,128)}, u32[]{:S(2)}) copy-start(s32[32,25,16,128]{3,2,1,0:T(8,128)} %get-tuple-element.73.ranks_ref) | copy-start | bytes 19660804 | tf_op jit(solution)/shard_map/cond
